TPU v7x, 32 devices: a whole 2x2x4 slice. The times are simulated.
32 devices in a mesh: groups: 2 (over y), expert: 8 (over z, x), mp: 2 (over core).
Axes of the slice: x: 2, y: 2, z: 4, core: 2. Of those that a mesh axis runs over, the one named last changes fastest.
Arguments:
- tokens: bfloat16 [64, 6144], P(('groups', 'expert', 'mp')), parts along dimension 0, may hold values from -6 to 6
- expert_ids: int32 [64, 2], P(('groups', 'expert', 'mp')), parts along dimension 0, may hold values from 0 to 3, all different within a row; in each aligned block of 2 rows (0 to 1, 2 to 3, ...) at most 2 rows name the same one
- mix_weights: float32 [64, 2], P(('groups', 'expert', 'mp')), parts along dimension 0, may hold values from 0.2 to 1
- w_gate: bfloat16 [6144, 32768], P(None, ('expert', 'mp')), may hold values from -0.078125 to 0.078125
- w_up: bfloat16 [6144, 32768], P(None, ('expert', 'mp')), may hold values from -0.078125 to 0.078125
- w_down: bfloat16 [32768, 6144], P(('expert', 'mp')), may hold values from -0.0625 to 0.0625
Outputs:
- combined: bfloat16 [64, 6144], P(('groups', 'expert', 'mp')), parts along dimension 0
There are 2 independent parts, one for each index of `groups`. A program takes and returns all parts, laid end to end along the dimension named above; an argument that names none is the same for every part. Nothing has to cross between parts.
Inputs may be any that keep to these rules, and one draw needn't show every extreme that they name: `expert_ids`: each row names two different experts. Among the rows of one device no expert is named more than 2 times, and in every draw some device names some expert exactly 2 times.
All inputs are finite; a program needn't handle non-finite values.
Results may differ from a plain program's by a relative error of at most 0.0081.
Values may be sent and summed in bfloat16 or wider, within the bound.
A program may use at most 128 MiB of HBM per device.

v0:
```python
import jax
import jax.numpy as jnp
from jax import lax
from jax.sharding import PartitionSpec as P

EXPERTS = 4
CAP = 2


def feed_forward(arrived_rows, gate_cols, up_cols, down_rows):
    layout = arrived_rows.shape
    flat_rows = arrived_rows.reshape(-1, layout[-1])
    gate_part = jnp.dot(flat_rows, gate_cols, preferred_element_type=jnp.float32)
    up_part = jnp.dot(flat_rows, up_cols, preferred_element_type=jnp.float32)
    hidden = (jax.nn.silu(gate_part) * up_part).astype(jnp.bfloat16)
    partial_value = jnp.dot(hidden, down_rows, preferred_element_type=jnp.float32)
    return partial_value.reshape(layout)


def send_back(partial_value):
    return lax.all_to_all(partial_value, "expert", split_axis=1, concat_axis=0, tiled=True)


def per_device(tokens, expert_ids, mix_weights, w_gate, w_up, w_down):
    shards = lax.axis_size("expert")
    owners = shards // EXPERTS
    tok_rows = tokens.shape[0]
    model_dim = tokens.shape[1]
    expert_range = jnp.arange(EXPERTS, dtype=jnp.int32)
    slot_count = EXPERTS * CAP
    flat_ids = expert_ids.reshape(-1)
    onehot = (flat_ids[:, None] == expert_range[None, :]).astype(jnp.int32)
    earlier = jnp.cumsum(onehot, axis=0) - onehot
    position = flat_ids * CAP + jnp.sum(earlier * onehot, axis=1)
    slot_map = (position[:, None] == jnp.arange(slot_count, dtype=jnp.int32)[None, :]).astype(
        jnp.float32
    )
    slot_map = slot_map.reshape(tok_rows, 2, slot_count)
    token_map = jnp.sum(slot_map, axis=1)
    combine = jnp.sum(slot_map * mix_weights[:, :, None], axis=1)
    compact = jnp.dot(
        token_map.T.astype(jnp.bfloat16), tokens, preferred_element_type=jnp.float32
    ).astype(jnp.bfloat16)
    outgoing = jnp.broadcast_to(
        compact.reshape(EXPERTS, 1, CAP, model_dim), (EXPERTS, owners, CAP, model_dim)
    )
    outgoing = outgoing.reshape(shards, 1, CAP, model_dim)
    paired = lax.all_gather(
        lax.all_to_all(outgoing, "expert", split_axis=0, concat_axis=1, tiled=True),
        "mp",
        axis=0,
        tiled=True,
    )
    partial_value = feed_forward(paired, w_gate, w_up, w_down)
    own_rows = lax.psum_scatter(partial_value, "mp", scatter_dimension=0, tiled=True)
    returned = send_back(own_rows)
    per_expert = jnp.sum(returned.reshape(EXPERTS, owners, CAP, model_dim), axis=1).reshape(
        slot_count, model_dim
    )
    combined = jnp.dot(
        combine, per_expert, precision=lax.Precision.HIGHEST, preferred_element_type=jnp.float32
    )
    return combined.astype(jnp.bfloat16)


def solution(mesh):
    in_specs = (
        P(("groups", "expert", "mp"), None),
        P(("groups", "expert", "mp"), None),
        P(("groups", "expert", "mp"), None),
        P(None, ("expert", "mp")),
        P(None, ("expert", "mp")),
        P(("expert", "mp"), None),
    )
    out_specs = P(("groups", "expert", "mp"), None)
    return jax.shard_map(
        per_device, mesh=mesh, in_specs=in_specs, out_specs=out_specs, check_vma=False
    )
```

profile of v0, /device:TPU:0, one launch (start us, length us, event | category | flops | bytes accessed | tf_op | source)
XLA Modules:
  0.0 93.4 jit_solution(9660064105527126358)
XLA Ops:
  6.5 0.0 copy-start
  6.5 0.0 reduce-scatter.2.cloned.1.call-start
  6.5 0.8 eq.29
  7.3 0.1 fusion.8
  7.4 0.2 select_reduce_fusion.1
  7.6 0.1 reduce_sum.39
  7.7 0.7 multiply_add_fusion
  8.4 0.8 convert_reduce_fusion
  9.1 0.0 copy-done
  9.2 0.2 convolution_convert_fusion
  9.4 0.1 broadcast_in_dim.4
  9.5 0.1 broadcast_in_dim.5
  9.6 15.0 %all_to_all.21 = bf16[8,1,2,6144]{3,2,1,0:T(2,128)(2,1)S(1)} all-to-all(bf16[8,1,2,6144]{3,2,1,0:T(2,128)(2,1)S(1)} %bitcast.12), channel_id=1, replica_groups=mesh['groups'=2,'expert'=8,'mp'=2] {'expert'}, dimensions={0} | all-to-all | bytes 393216 | tf_op jit(solution)/shard_map/all_to_all | solution.py:49
  24.6 2.1 %all-gather = bf16[16,1,2,6144]{3,2,1,0:T(2,128)(2,1)S(1)} all-gather(bf16[8,1,2,6144]{3,2,1,0:T(2,128)(2,1)S(1)} %all_to_all.21), channel_id=2, replica_groups=mesh['groups'=2,'expert'=8,'mp'=2] {'mp'}, dimensions={0}, use_global_device_ids=true | all-gather | bytes 589824 | tf_op jit(solution)/shard_map/all_gather | solution.py:48
  26.7 0.1 reshape.45
  26.8 10.4 %fusion.11 = f32[32,2048]{1,0:T(8,128)S(1)} fusion(bf16[32,6144]{1,0:T(8,128)(2,1)S(1)} %reshape.45, bf16[6144,2048]{1,0:T(8,128)(2,1)} %param.9), kind=kOutput, calls=%fused_computation.20 | convolution fusion | flops 805306368 | bytes 25821184 | tf_op jit(solution)/shard_map/dot_general | solution.py:13
  37.3 19.8 %fusion.1 = f32[32,6144]{1,0:T(8,128)S(1)} fusion(bf16[2048,6144]{1,0:T(8,128)(2,1)} %param.11, bf16[32,6144]{1,0:T(8,128)(2,1)S(1)} %reshape.45, bf16[6144,2048]{1,0:T(8,128)(2,1)} %param.10, f32[32,2048]{1,0:T(8,128)S(1)} %fusion.11), kind=kOutput, calls=%fused_computation.4 | convolution fusion | flops 1611005952 | bytes 51773440 | tf_op jit(solution)/shard_map/dot_general | solution.py:16
  57.1 0.5 reshape.46
  57.6 1.3 %copy.9 = f32[2,8,2,6144]{3,1,2,0:T(8,128)} copy(f32[2,8,2,6144]{3,2,1,0:T(2,128)S(1)} %reshape.46) | data formatting | bytes 1572864 | tf_op jit(solution)/shard_map/reshape | solution.py:17
  58.9 0.0 reduce-scatter.2.cloned.1.call-update
  58.9 6.9 %reduce-scatter.2.cloned.1.call-done = f32[1,8,2,6144]{3,1,2,0:T(8,128)} async-done(((f32[2,8,2,6144]{3,1,2,0:T(8,128)}), f32[1,8,2,6144]{3,1,2,0:T(8,128)}) %reduce-scatter.2.cloned.1.call-update) | async-done | bytes 393232 | tf_op jit(solution)/shard_map/reduce_scatter | solution.py:55
  65.8 1.3 %copy.10 = f32[1,8,2,6144]{3,2,0,1:T(2,128)S(1)} copy(f32[1,8,2,6144]{3,1,2,0:T(8,128)} %reduce-scatter.2.cloned.1.call-done) | data formatting | bytes 786432 | tf_op jit(solution)/shard_map/reduce_scatter | solution.py:55
  67.2 18.1 %all_to_all.22 = f32[1,8,2,6144]{3,2,0,1:T(2,128)S(1)} all-to-all(f32[1,8,2,6144]{3,2,0,1:T(2,128)S(1)} %copy.10), channel_id=1, replica_groups=mesh['groups'=2,'expert'=8,'mp'=2] {'expert'}, dimensions={1} | all-to-all | bytes 786432 | tf_op jit(solution)/shard_map/all_to_all | solution.py:21
  85.2 0.3 reduce_sum.42
  85.5 0.1 reshape.48
  85.7 0.9 convolution_convert_fusion.1
  (1 shorter events, 0.0 us)
Async XLA Ops:
  6.5 2.6 %copy-start = (bf16[2,6144]{1,0:T(2,128)(2,1)S(1)}, bf16[2,6144]{1,0:T(2,128)(2,1)}, u32[]{:S(2)}) copy-start(bf16[2,6144]{1,0:T(2,128)(2,1)} %param.6) | copy-start | bytes 73732
  6.5 59.3 %reduce-scatter.2.cloned.1.call-start = ((), (), s32[]{:S(2)}) async-start(), calls=%async_computation.3 | async-start | bytes 1179648 | tf_op jit(solution)/shard_map/reduce_scatter | solution.py:55
Sparse Core Ops, SparseCore 0:
  59.1 6.7 reduce-scatter.1
where the time goes:
time: 93.8 us; the launch traced here: 93.4 us
  blocking collectives  35.2 us (38%)
  matrix products  31.4 us (33%)
  between operations  13.4 us (14%)
  waiting for transfers between devices  6.93 us (7%)
  local copies, waits for them, and re-layouts  4.43 us (5%)
  other arithmetic  2.04 us (2%)
    dot_general x1, matrix products, feed_forward(): jnp.dot(hidden, down_rows, preferred_element_type=jnp.float32)  19.8 us
    all_to_all x1, blocking collectives, send_back(): lax.all_to_all(partial_value, 'expert', split_axis=1, concat_axis=0, tile...  18.1 us
    all_to_all x1, blocking collectives, per_device(): lax.all_to_all(outgoing, 'expert', split_axis=0, concat_axis=1, tiled=True)  15 us
    dot_general x1, matrix products, feed_forward(): jnp.dot(flat_rows, gate_cols, preferred_element_type=jnp.float32)  10.4 us
    reduce_scatter x1, waiting for transfers between devices, per_device(): lax.psum_scatter(partial_value, 'mp', scatter_dimension=0, tiled=True)  6.92 us
    all_gather x1, blocking collectives, per_device(): lax.all_gather(lax.all_to_all(outgoing, 'expert', split_axis=0, concat_ax...  2.08 us
  transfers between devices with their start and end apart: 1, of which 1 were waited for; matrix products, arithmetic and copies ran while one was open for 0% of the time, Pallas kernels for 0%

commit v1 on v0

v1 whole, which is shorter than its diff:
```python
import functools

import jax
import jax.numpy as jnp
from jax import lax
from jax.experimental import pallas as pl
from jax.experimental.pallas import tpu as pltpu
from jax.sharding import PartitionSpec as P

EXPERTS = 4
SLOT_BUDGET = 58 * 1024 * 1024
VMEM_LIMIT = 67043328
EARLY = 6
LAG = 2
MESH = pl.DeviceIdType.MESH


def block_of(extent, most):
    size = min(extent, most)
    while extent % size:
        size //= 2
    return size


def kernel(
    shards, cores, plan,
    ids_ref, mix_ref, tok_ref, gate_ref, up_ref, down_ref, out_ref,
    slots, arrived, rows_ref, hidden_ref, outbox, inbox,
    slot_sem, tok_send, tok_recv, own_sem, part_send, part_recv,
):
    kg, ng, kd, nd, depth = plan
    model_dim, units = gate_ref.shape
    count = shards * cores
    tok_rows = tok_ref.shape[0]
    rows = count * tok_rows
    k_blocks, n_blocks, out_blocks = model_dim // kg, units // ng, model_dim // nd
    first_total = n_blocks * k_blocks * 2
    total = first_total + out_blocks
    me = lax.axis_index("expert") * cores + lax.axis_index("mp")

    def where(peer):
        return {"expert": peer // cores, "mp": lax.rem(peer, cores)}

    def peer_at(step):
        return lax.rem(me + step, count)

    barrier = pltpu.get_barrier_semaphore()

    @pl.loop(1, count)
    def _(step):
        pl.semaphore_signal(barrier, inc=1, device_id=where(peer_at(step)), device_id_type=MESH)

    def gate_copy(c, source):
        pair = c // 2
        n, k = pair // k_blocks, lax.rem(pair, k_blocks)
        slot = lax.rem(c, depth)
        return pltpu.make_async_copy(
            source.at[pl.ds(pl.multiple_of(k * kg, kg), kg), pl.ds(pl.multiple_of(n * ng, ng), ng)],
            slots.at[slot, pl.ds(0, kg), pl.ds(0, ng)],
            slot_sem.at[slot],
        )

    def down_copy(c):
        slot = lax.rem(c, depth)
        col = (c - first_total) * nd
        return pltpu.make_async_copy(
            down_ref.at[:, pl.ds(pl.multiple_of(col, nd), nd)],
            slots.at[slot, pl.ds(0, kd), pl.ds(0, nd)],
            slot_sem.at[slot],
        )

    def start_chunk(c):
        odd = lax.rem(c, 2)

        @pl.when((c < first_total) & (odd == 0))
        def _():
            gate_copy(c, gate_ref).start()

        @pl.when((c < first_total) & (odd == 1))
        def _():
            gate_copy(c, up_ref).start()

        @pl.when((c >= first_total) & (c < total))
        def _():
            down_copy(c).start()

    early = min(EARLY, depth)

    @pl.loop(0, early)
    def _(c):
        start_chunk(c)

    own = pltpu.make_async_copy(tok_ref, arrived.at[me], own_sem)
    own.start()
    pl.semaphore_wait(barrier, count - 1)

    def token_copy(step):
        return pltpu.make_async_remote_copy(
            src_ref=tok_ref, dst_ref=arrived.at[me], send_sem=tok_send, recv_sem=tok_recv,
            device_id=where(peer_at(step)), device_id_type=MESH,
        )

    @pl.loop(1, count)
    def _(step):
        token_copy(step).start()

    @pl.loop(early, depth)
    def _(c):
        start_chunk(c)

    own.wait()
    others = arrived.at[pl.ds(0, count - 1)]
    pltpu.make_async_copy(others, others, tok_recv).wait()

    group = 16 // tok_rows

    @pl.loop(0, count // group)
    def _(g):
        pieces = [arrived[g * group + j] for j in range(group)]
        rows_ref[pl.ds(pl.multiple_of(g * 16, 16), 16), :] = jnp.concatenate(pieces, axis=0)

    @pl.loop(0, n_blocks)
    def _(n):
        sums = [jnp.zeros((rows, ng), jnp.float32), jnp.zeros((rows, ng), jnp.float32)]
        for k in range(k_blocks):
            for side in range(2):
                c = (n * k_blocks + k) * 2 + side
                slot = lax.rem(c, depth)
                gate_copy(c, (gate_ref, up_ref)[side]).wait()
                sums[side] = sums[side] + jnp.dot(
                    rows_ref[:, k * kg:(k + 1) * kg],
                    slots[slot, pl.ds(0, kg), pl.ds(0, ng)],
                    preferred_element_type=jnp.float32,
                )
                start_chunk(c + depth)
        hidden = (jax.nn.silu(sums[0]) * sums[1]).astype(jnp.bfloat16)
        hidden_ref[:, pl.ds(pl.multiple_of(n * ng, ng), ng)] = hidden

    def part_copy(block, step):
        cols = pl.ds(pl.multiple_of(block * nd, nd), nd)
        peer = peer_at(step)
        return pltpu.make_async_remote_copy(
            src_ref=outbox.at[peer, :, cols], dst_ref=inbox.at[me, :, cols],
            send_sem=part_send.at[block], recv_sem=part_recv.at[block],
            device_id=where(peer), device_id_type=MESH,
        )

    per = count // EXPERTS
    row_at = lax.broadcasted_iota(jnp.int32, (tok_rows, nd), 0)

    def combine(block):
        cols = pl.ds(pl.multiple_of(block * nd, nd), nd)
        landed = inbox.at[pl.ds(0, count - 1), :, cols]
        pltpu.make_async_copy(landed, landed, part_recv.at[block]).wait()
        result = jnp.zeros((tok_rows, nd), jnp.float32)
        for expert in range(EXPERTS):
            weight = jnp.zeros((tok_rows, nd), jnp.float32)
            for t in range(tok_rows):
                scale = jnp.float32(0.0)
                for k in range(ids_ref.shape[1]):
                    scale = scale + jnp.where(ids_ref[t, k] == expert, mix_ref[t, k], 0.0)
                weight = jnp.where(row_at == t, scale, weight)
            value = lax.fori_loop(
                0, per,
                lambda i, s: s + inbox[expert * per + i, :, cols].astype(jnp.float32),
                jnp.zeros((tok_rows, nd), jnp.float32),
                unroll=per <= 8,
            )
            result = result + weight * value
        out_ref[:, cols] = result.astype(out_ref.dtype)

    @pl.loop(0, out_blocks)
    def _(block):
        c = first_total + block
        cols = pl.ds(pl.multiple_of(block * nd, nd), nd)
        down_copy(c).wait()
        part = jnp.dot(
            hidden_ref[...], slots[lax.rem(c, depth), pl.ds(0, kd), pl.ds(0, nd)],
            preferred_element_type=jnp.float32,
        ).astype(jnp.bfloat16)
        start_chunk(c + depth)
        for p in range(count):
            outbox[p, :, cols] = part[p * tok_rows:(p + 1) * tok_rows, :]
        inbox[me, :, cols] = outbox[me, :, cols]

        @pl.loop(1, count)
        def _(step):
            part_copy(block, step).start()

        @pl.when(block >= LAG)
        def _():
            combine(block - LAG)

    @pl.loop(out_blocks - LAG, out_blocks)
    def _(block):
        combine(block)

    pltpu.make_async_copy(others, others, tok_send).wait()

    @pl.loop(0, out_blocks)
    def _(block):
        left = outbox.at[pl.ds(0, count - 1), :, pl.ds(pl.multiple_of(block * nd, nd), nd)]
        pltpu.make_async_copy(left, left, part_send.at[block]).wait()


def per_device(tokens, expert_ids, mix_weights, w_gate, w_up, w_down):
    shards, cores = lax.axis_size("expert"), lax.axis_size("mp")
    count = shards * cores
    tok_rows, model_dim = tokens.shape
    units = w_gate.shape[1]
    kg, ng = block_of(model_dim, 2048), block_of(units, 512)
    kd, nd = units, block_of(model_dim, 512)
    slot_shape = (max(kg, kd), max(ng, nd))
    chunks = (model_dim // kg) * (units // ng) * 2 + model_dim // nd
    kept = 4 * count * tok_rows * model_dim * 2
    depth = min(chunks, (SLOT_BUDGET - kept) // (slot_shape[0] * slot_shape[1] * 2))
    vmem = pl.BlockSpec(memory_space=pltpu.VMEM)
    smem = pl.BlockSpec(memory_space=pltpu.SMEM)
    hbm = pl.BlockSpec(memory_space=pl.ANY)
    boxes = (count, tok_rows, model_dim)
    return pl.pallas_call(
        functools.partial(kernel, shards, cores, (kg, ng, kd, nd, depth)),
        out_shape=jax.ShapeDtypeStruct((tok_rows, model_dim), jnp.bfloat16),
        in_specs=[smem, smem, vmem, hbm, hbm, hbm],
        out_specs=vmem,
        scratch_shapes=[
            pltpu.VMEM((depth, *slot_shape), jnp.bfloat16),
            pltpu.VMEM(boxes, jnp.bfloat16),
            pltpu.VMEM((count * tok_rows, model_dim), jnp.bfloat16),
            pltpu.VMEM((count * tok_rows, units), jnp.bfloat16),
            pltpu.VMEM(boxes, jnp.bfloat16),
            pltpu.VMEM(boxes, jnp.bfloat16),
            pltpu.SemaphoreType.DMA((depth,)),
            pltpu.SemaphoreType.DMA,
            pltpu.SemaphoreType.DMA,
            pltpu.SemaphoreType.DMA,
            pltpu.SemaphoreType.DMA((model_dim // nd,)),
            pltpu.SemaphoreType.DMA((model_dim // nd,)),
        ],
        compiler_params=pltpu.CompilerParams(
            collective_id=0, has_side_effects=True, vmem_limit_bytes=VMEM_LIMIT
        ),
    )(expert_ids, mix_weights, tokens, w_gate, w_up, w_down)


def solution(mesh):
    in_specs = (
        P(("groups", "expert", "mp"), None),
        P(("groups", "expert", "mp"), None),
        P(("groups", "expert", "mp"), None),
        P(None, ("expert", "mp")),
        P(None, ("expert", "mp")),
        P(("expert", "mp"), None),
    )
    out_specs = P(("groups", "expert", "mp"), None)
    return jax.shard_map(
        per_device, mesh=mesh, in_specs=in_specs, out_specs=out_specs, check_vma=False
    )
```

time: 93.8 us -> 49.6 us (0.53)
  Pallas kernels: 0 us -> 48 us
  blocking collectives: 35.2 us -> 0 us
  matrix products: 31.4 us -> 0 us
  between operations: 13.4 us -> 0.01 us
  waiting for transfers between devices: 6.93 us -> 0 us
  local copies, waits for them, and re-layouts: 4.43 us -> 1.36 us
  other arithmetic: 2.04 us -> 0 us
    pallas_call x0 -> x1, Pallas kernels: none -> 48 us  [per_device(): pl.pallas_call(functools.partial(kernel, shards, cores, (kg, ng, kd, nd,...]
    all_to_all x2 -> x0, blocking collectives: 33.1 us -> none  [the longest x1 18.1 us: send_back(): lax.all_to_all(partial_value, 'expert', split_axis=1, concat_axis=0, tile...]
    dot_general x4 -> x0, matrix products: 31.4 us -> none  [the longest x1 19.8 us: feed_forward(): jnp.dot(hidden, down_rows, preferred_element_type=jnp.float32)]
    reduce_scatter x1 -> x0, waiting for transfers between devices: 6.92 us -> none  [per_device(): lax.psum_scatter(partial_value, 'mp', scatter_dimension=0, tiled=True)]
    reshape x4 -> x0, local copies, waits for them, and re-layouts: 2.08 us -> none  [the longest x2 1.8 us: feed_forward(): return partial_value.reshape(layout)]
    all_gather x1 -> x0, blocking collectives: 2.08 us -> none  [per_device(): lax.all_gather(lax.all_to_all(outgoing, 'expert', split_axis=0, concat_ax...]
    unnamed x2 -> x1, local copies, waits for them, and re-layouts: 0.01 us -> 1.36 us
    reduce_scatter x1 -> x0, local copies, waits for them, and re-layouts: 1.3 us -> none  [per_device(): lax.psum_scatter(partial_value, 'mp', scatter_dimension=0, tiled=True)]
  transfers between devices with their start and end apart: 1 -> 0, of which waited for: 1 -> 0; matrix products, arithmetic and copies ran while one was open for 0% -> 0% of each run, Pallas kernels for 0% -> 0%
where the time goes in v1:
time: 49.6 us; the launch traced here: 49.4 us
  Pallas kernels  48 us (97%)
  local copies, waits for them, and re-layouts  1.36 us (3%)
    pallas_call x1, Pallas kernels, per_device(): pl.pallas_call(functools.partial(kernel, shards, cores, (kg, ng, kd, nd,...  48 us
    unnamed x1, local copies, waits for them, and re-layouts  1.36 us

profile of v1, /device:TPU:0, one launch (start us, length us, event | category | flops | bytes accessed | tf_op | source)
XLA Modules:
  0.0 49.4 jit_solution(7592208578386027420)
XLA Ops:
  0.0 48.0 %shard_map.64 = bf16[2,6144]{1,0:T(2,128)(2,1)} custom-call(s32[2,2]{1,0:T(2,128)} %ids_ref.1, f32[2,2]{1,0:T(2,128)} %mix_ref.1, bf16[2,6144]{1,0:T(2,128)(2,1)} %tok_ref.1, bf16[6144,2048]{1,0:T(8,128)(2,1)} %gate_ref.1, bf16[6144,2048]{1,0:T(8,128)(2,1)} %up_ref.1, bf16[2048,6144]{1,0:T(8,128)(2,1)} %down_ref.1), custom_call_target="tpu_custom_call" | custom-call | tf_op jit(solution)/shard_map/pallas_call | solution.py:221
  48.0 1.4 %copy.8 = bf16[2,6144]{1,0:T(2,128)(2,1)} copy(bf16[2,6144]{1,0:T(2,128)(2,1)} %shard_map.64) | data formatting | bytes 49152

commit v2 on v1

--- a/solution.py
+++ b/solution.py
@@ -11,7 +11,8 @@
 SLOT_BUDGET = 58 * 1024 * 1024
 VMEM_LIMIT = 67043328
 EARLY = 6
-LAG = 2
+HOP = 1
+LAG = 5
 MESH = pl.DeviceIdType.MESH
 
 
@@ -25,8 +26,9 @@
 def kernel(
     shards, cores, plan,
     ids_ref, mix_ref, tok_ref, gate_ref, up_ref, down_ref, out_ref,
-    slots, arrived, rows_ref, hidden_ref, outbox, inbox,
-    slot_sem, tok_send, tok_recv, own_sem, part_send, part_recv,
+    slots, arrived, rows_ref, hidden_ref, outbox, corebox, sumbox, inbox,
+    slot_sem, tok_send, tok_recv, own_sem, pass_send, pass_recv,
+    core_send, core_recv, part_send, part_recv,
 ):
     kg, ng, kd, nd, depth = plan
     model_dim, units = gate_ref.shape
@@ -36,19 +38,24 @@
     k_blocks, n_blocks, out_blocks = model_dim // kg, units // ng, model_dim // nd
     first_total = n_blocks * k_blocks * 2
     total = first_total + out_blocks
-    me = lax.axis_index("expert") * cores + lax.axis_index("mp")
-
-    def where(peer):
-        return {"expert": peer // cores, "mp": lax.rem(peer, cores)}
-
-    def peer_at(step):
-        return lax.rem(me + step, count)
+    shard, core = lax.axis_index("expert"), lax.axis_index("mp")
+
+    def shard_at(step):
+        return lax.rem(shard + step, shards)
+
+    def core_at(step):
+        return lax.rem(core + step, cores)
 
     barrier = pltpu.get_barrier_semaphore()
 
-    @pl.loop(1, count)
+    for step in range(1, cores):
+        pl.semaphore_signal(barrier, inc=1, device_id={"mp": core_at(step)}, device_id_type=MESH)
+
+    @pl.loop(1, shards)
     def _(step):
-        pl.semaphore_signal(barrier, inc=1, device_id=where(peer_at(step)), device_id_type=MESH)
+        pl.semaphore_signal(
+            barrier, inc=1, device_id={"expert": shard_at(step)}, device_id_type=MESH
+        )
 
     def gate_copy(c, source):
         pair = c // 2
@@ -90,33 +97,53 @@
     def _(c):
         start_chunk(c)
 
-    own = pltpu.make_async_copy(tok_ref, arrived.at[me], own_sem)
+    own = pltpu.make_async_copy(tok_ref, arrived.at[core, shard], own_sem)
     own.start()
-    pl.semaphore_wait(barrier, count - 1)
-
-    def token_copy(step):
+    pl.semaphore_wait(barrier, shards + cores - 2)
+
+    def token_copy(step, source):
         return pltpu.make_async_remote_copy(
-            src_ref=tok_ref, dst_ref=arrived.at[me], send_sem=tok_send, recv_sem=tok_recv,
-            device_id=where(peer_at(step)), device_id_type=MESH,
-        )
-
-    @pl.loop(1, count)
+            src_ref=tok_ref, dst_ref=arrived.at[core, shard],
+            send_sem=tok_send, recv_sem=tok_recv.at[source],
+            device_id={"expert": shard_at(step)}, device_id_type=MESH,
+        )
+
+    def pass_on(source, step, from_ref):
+        return pltpu.make_async_remote_copy(
+            src_ref=from_ref, dst_ref=arrived.at[core, source],
+            send_sem=pass_send, recv_sem=pass_recv,
+            device_id={"mp": core_at(step)}, device_id_type=MESH,
+        )
+
+    @pl.loop(1, shards)
     def _(step):
-        token_copy(step).start()
+        token_copy(step, shard).start()
+
+    for step in range(1, cores):
+        pass_on(shard, step, tok_ref).start()
 
     @pl.loop(early, depth)
     def _(c):
         start_chunk(c)
 
+    @pl.loop(1, shards)
+    def _(step):
+        source = lax.rem(shard + shards - step, shards)
+        token_copy(step, source).wait_recv()
+        for other in range(1, cores):
+            pass_on(source, other, arrived.at[core, source]).start()
+
     own.wait()
-    others = arrived.at[pl.ds(0, count - 1)]
-    pltpu.make_async_copy(others, others, tok_recv).wait()
+    for step in range(1, cores):
+        whole = arrived.at[core_at(step)]
+        pltpu.make_async_copy(whole, whole, pass_recv).wait()
 
     group = 16 // tok_rows
 
     @pl.loop(0, count // group)
     def _(g):
-        pieces = [arrived[g * group + j] for j in range(group)]
+        flat = [g * group + j for j in range(group)]
+        pieces = [arrived[i // shards, lax.rem(i, shards)] for i in flat]
         rows_ref[pl.ds(pl.multiple_of(g * 16, 16), 16), :] = jnp.concatenate(pieces, axis=0)
 
     @pl.loop(0, n_blocks)
@@ -136,21 +163,51 @@
         hidden = (jax.nn.silu(sums[0]) * sums[1]).astype(jnp.bfloat16)
         hidden_ref[:, pl.ds(pl.multiple_of(n * ng, ng), ng)] = hidden
 
+    def cols_of(block):
+        return pl.ds(pl.multiple_of(block * nd, nd), nd)
+
+    def core_copy(block, step):
+        return pltpu.make_async_remote_copy(
+            src_ref=outbox.at[core_at(step), :, :, cols_of(block)],
+            dst_ref=corebox.at[core, :, :, cols_of(block)],
+            send_sem=core_send.at[block], recv_sem=core_recv.at[block],
+            device_id={"mp": core_at(step)}, device_id_type=MESH,
+        )
+
     def part_copy(block, step):
-        cols = pl.ds(pl.multiple_of(block * nd, nd), nd)
-        peer = peer_at(step)
+        peer = shard_at(step)
         return pltpu.make_async_remote_copy(
-            src_ref=outbox.at[peer, :, cols], dst_ref=inbox.at[me, :, cols],
+            src_ref=sumbox.at[peer, :, cols_of(block)],
+            dst_ref=inbox.at[shard, :, cols_of(block)],
             send_sem=part_send.at[block], recv_sem=part_recv.at[block],
-            device_id=where(peer), device_id_type=MESH,
-        )
-
-    per = count // EXPERTS
+            device_id={"expert": peer}, device_id_type=MESH,
+        )
+
+    def exchange(block):
+        cols = cols_of(block)
+        landed = corebox.at[pl.ds(0, cores - 1), :, :, cols]
+        pltpu.make_async_copy(landed, landed, core_recv.at[block]).wait()
+
+        def add_up(owner, carry):
+            value = outbox[core, owner, :, cols].astype(jnp.float32)
+            for step in range(1, cores):
+                value = value + corebox[core_at(step), owner, :, cols].astype(jnp.float32)
+            sumbox[owner, :, cols] = value.astype(jnp.bfloat16)
+            return carry
+
+        lax.fori_loop(0, shards, add_up, 0, unroll=shards <= 8)
+        inbox[shard, :, cols] = sumbox[shard, :, cols]
+
+        @pl.loop(1, shards)
+        def _(step):
+            part_copy(block, step).start()
+
+    per = shards // EXPERTS
     row_at = lax.broadcasted_iota(jnp.int32, (tok_rows, nd), 0)
 
     def combine(block):
-        cols = pl.ds(pl.multiple_of(block * nd, nd), nd)
-        landed = inbox.at[pl.ds(0, count - 1), :, cols]
+        cols = cols_of(block)
+        landed = inbox.at[pl.ds(0, shards - 1), :, cols]
         pltpu.make_async_copy(landed, landed, part_recv.at[block]).wait()
         result = jnp.zeros((tok_rows, nd), jnp.float32)
         for expert in range(EXPERTS):
@@ -172,7 +229,7 @@
     @pl.loop(0, out_blocks)
     def _(block):
         c = first_total + block
-        cols = pl.ds(pl.multiple_of(block * nd, nd), nd)
+        cols = cols_of(block)
         down_copy(c).wait()
         part = jnp.dot(
             hidden_ref[...], slots[lax.rem(c, depth), pl.ds(0, kd), pl.ds(0, nd)],
@@ -180,26 +237,33 @@
         ).astype(jnp.bfloat16)
         start_chunk(c + depth)
         for p in range(count):
-            outbox[p, :, cols] = part[p * tok_rows:(p + 1) * tok_rows, :]
-        inbox[me, :, cols] = outbox[me, :, cols]
-
-        @pl.loop(1, count)
-        def _(step):
-            part_copy(block, step).start()
+            outbox[p // shards, p % shards, :, cols] = part[p * tok_rows:(p + 1) * tok_rows, :]
+        for step in range(1, cores):
+            core_copy(block, step).start()
+
+        @pl.when(block >= HOP)
+        def _():
+            exchange(block - HOP)
 
         @pl.when(block >= LAG)
         def _():
             combine(block - LAG)
 
-    @pl.loop(out_blocks - LAG, out_blocks)
-    def _(block):
+    for block in range(max(out_blocks - HOP, 0), out_blocks):
+        exchange(block)
+    for block in range(max(out_blocks - LAG, 0), out_blocks):
         combine(block)
 
-    pltpu.make_async_copy(others, others, tok_send).wait()
+    tokens_out = arrived.at[0, pl.ds(0, shards - 1)]
+    pltpu.make_async_copy(tokens_out, tokens_out, tok_send).wait()
+    passed = arrived.at[pl.ds(0, cores - 1)]
+    pltpu.make_async_copy(passed, passed, pass_send).wait()
 
     @pl.loop(0, out_blocks)
     def _(block):
-        left = outbox.at[pl.ds(0, count - 1), :, pl.ds(pl.multiple_of(block * nd, nd), nd)]
+        left = outbox.at[pl.ds(0, cores - 1), :, :, cols_of(block)]
+        pltpu.make_async_copy(left, left, core_send.at[block]).wait()
+        left = sumbox.at[pl.ds(0, shards - 1), :, cols_of(block)]
         pltpu.make_async_copy(left, left, part_send.at[block]).wait()
 
 
@@ -212,12 +276,12 @@
     kd, nd = units, block_of(model_dim, 512)
     slot_shape = (max(kg, kd), max(ng, nd))
     chunks = (model_dim // kg) * (units // ng) * 2 + model_dim // nd
-    kept = 4 * count * tok_rows * model_dim * 2
+    kept = 5 * count * tok_rows * model_dim * 2
     depth = min(chunks, (SLOT_BUDGET - kept) // (slot_shape[0] * slot_shape[1] * 2))
     vmem = pl.BlockSpec(memory_space=pltpu.VMEM)
     smem = pl.BlockSpec(memory_space=pltpu.SMEM)
     hbm = pl.BlockSpec(memory_space=pl.ANY)
-    boxes = (count, tok_rows, model_dim)
+    boxes = (cores, shards, tok_rows, model_dim)
     return pl.pallas_call(
         functools.partial(kernel, shards, cores, (kg, ng, kd, nd, depth)),
         out_shape=jax.ShapeDtypeStruct((tok_rows, model_dim), jnp.bfloat16),
@@ -230,12 +294,15 @@
             pltpu.VMEM((count * tok_rows, units), jnp.bfloat16),
             pltpu.VMEM(boxes, jnp.bfloat16),
             pltpu.VMEM(boxes, jnp.bfloat16),
+            pltpu.VMEM(boxes[1:], jnp.bfloat16),
+            pltpu.VMEM(boxes[1:], jnp.bfloat16),
             pltpu.SemaphoreType.DMA((depth,)),
+            pltpu.SemaphoreType.DMA,
+            pltpu.SemaphoreType.DMA((shards,)),
             pltpu.SemaphoreType.DMA,
             pltpu.SemaphoreType.DMA,
             pltpu.SemaphoreType.DMA,
-            pltpu.SemaphoreType.DMA((model_dim // nd,)),
-            pltpu.SemaphoreType.DMA((model_dim // nd,)),
+            *[pltpu.SemaphoreType.DMA((model_dim // nd,))] * 4,
         ],
         compiler_params=pltpu.CompilerParams(
             collective_id=0, has_side_effects=True, vmem_limit_bytes=VMEM_LIMIT

time: 49.6 us -> 42.6 us (0.86)
  Pallas kernels: 48 us -> 41 us
    pallas_call x1, Pallas kernels: 48 us -> 41 us  [per_device(): pl.pallas_call(functools.partial(kernel, shards, cores, (kg, ng, kd, nd,...]
where the time goes in v2:
time: 42.6 us; the launch traced here: 42.4 us
  Pallas kernels  41 us (96%)
  local copies, waits for them, and re-layouts  1.36 us (3%)
    pallas_call x1, Pallas kernels, per_device(): pl.pallas_call(functools.partial(kernel, shards, cores, (kg, ng, kd, nd,...  41 us
    unnamed x1, local copies, waits for them, and re-layouts  1.36 us

profile of v2, /device:TPU:0, one launch (start us, length us, event | category | flops | bytes accessed | tf_op | source)
XLA Modules:
  0.0 42.4 jit_solution(15367389042514501748)
XLA Ops:
  0.0 41.0 %shard_map.64 = bf16[2,6144]{1,0:T(2,128)(2,1)} custom-call(s32[2,2]{1,0:T(2,128)} %ids_ref.1, f32[2,2]{1,0:T(2,128)} %mix_ref.1, bf16[2,6144]{1,0:T(2,128)(2,1)} %tok_ref.1, bf16[6144,2048]{1,0:T(8,128)(2,1)} %gate_ref.1, bf16[6144,2048]{1,0:T(8,128)(2,1)} %up_ref.1, bf16[2048,6144]{1,0:T(8,128)(2,1)} %down_ref.1), custom_call_target="tpu_custom_call" | custom-call | tf_op jit(solution)/shard_map/pallas_call | solution.py:285
  41.0 1.4 %copy.8 = bf16[2,6144]{1,0:T(2,128)(2,1)} copy(bf16[2,6144]{1,0:T(2,128)(2,1)} %shard_map.64) | data formatting | bytes 49152

commit v3 on v2

--- a/solution.py
+++ b/solution.py
@@ -11,8 +11,8 @@
 SLOT_BUDGET = 58 * 1024 * 1024
 VMEM_LIMIT = 67043328
 EARLY = 6
-HOP = 1
-LAG = 5
+HOP = 2
+LAG = 8
 MESH = pl.DeviceIdType.MESH
 
 
@@ -168,8 +168,8 @@
 
     def core_copy(block, step):
         return pltpu.make_async_remote_copy(
-            src_ref=outbox.at[core_at(step), :, :, cols_of(block)],
-            dst_ref=corebox.at[core, :, :, cols_of(block)],
+            src_ref=outbox.at[core_at(step), :, cols_of(block)],
+            dst_ref=corebox.at[core, :, cols_of(block)],
             send_sem=core_send.at[block], recv_sem=core_recv.at[block],
             device_id={"mp": core_at(step)}, device_id_type=MESH,
         )
@@ -185,17 +185,15 @@
 
     def exchange(block):
         cols = cols_of(block)
-        landed = corebox.at[pl.ds(0, cores - 1), :, :, cols]
+        landed = corebox.at[pl.ds(0, cores - 1), :, cols]
         pltpu.make_async_copy(landed, landed, core_recv.at[block]).wait()
 
-        def add_up(owner, carry):
-            value = outbox[core, owner, :, cols].astype(jnp.float32)
-            for step in range(1, cores):
-                value = value + corebox[core_at(step), owner, :, cols].astype(jnp.float32)
-            sumbox[owner, :, cols] = value.astype(jnp.bfloat16)
-            return carry
-
-        lax.fori_loop(0, shards, add_up, 0, unroll=shards <= 8)
+        value = outbox[core, :, cols].astype(jnp.float32)
+        for step in range(1, cores):
+            value = value + corebox[core_at(step), :, cols].astype(jnp.float32)
+        value = value.astype(jnp.bfloat16)
+        for owner in range(shards):
+            sumbox[owner, :, cols] = value[owner * tok_rows:(owner + 1) * tok_rows, :]
         inbox[shard, :, cols] = sumbox[shard, :, cols]
 
         @pl.loop(1, shards)
@@ -236,8 +234,9 @@
             preferred_element_type=jnp.float32,
         ).astype(jnp.bfloat16)
         start_chunk(c + depth)
-        for p in range(count):
-            outbox[p // shards, p % shards, :, cols] = part[p * tok_rows:(p + 1) * tok_rows, :]
+        half = shards * tok_rows
+        for side in range(cores):
+            outbox[side, :, cols] = part[side * half:(side + 1) * half, :]
         for step in range(1, cores):
             core_copy(block, step).start()
 
@@ -261,7 +260,7 @@
 
     @pl.loop(0, out_blocks)
     def _(block):
-        left = outbox.at[pl.ds(0, cores - 1), :, :, cols_of(block)]
+        left = outbox.at[pl.ds(0, cores - 1), :, cols_of(block)]
         pltpu.make_async_copy(left, left, core_send.at[block]).wait()
         left = sumbox.at[pl.ds(0, shards - 1), :, cols_of(block)]
         pltpu.make_async_copy(left, left, part_send.at[block]).wait()
@@ -282,6 +281,7 @@
     smem = pl.BlockSpec(memory_space=pltpu.SMEM)
     hbm = pl.BlockSpec(memory_space=pl.ANY)
     boxes = (cores, shards, tok_rows, model_dim)
+    halves = (cores, shards * tok_rows, model_dim)
     return pl.pallas_call(
         functools.partial(kernel, shards, cores, (kg, ng, kd, nd, depth)),
         out_shape=jax.ShapeDtypeStruct((tok_rows, model_dim), jnp.bfloat16),
@@ -292,8 +292,8 @@
             pltpu.VMEM(boxes, jnp.bfloat16),
             pltpu.VMEM((count * tok_rows, model_dim), jnp.bfloat16),
             pltpu.VMEM((count * tok_rows, units), jnp.bfloat16),
-            pltpu.VMEM(boxes, jnp.bfloat16),
-            pltpu.VMEM(boxes, jnp.bfloat16),
+            pltpu.VMEM(halves, jnp.bfloat16),
+            pltpu.VMEM(halves, jnp.bfloat16),
             pltpu.VMEM(boxes[1:], jnp.bfloat16),
             pltpu.VMEM(boxes[1:], jnp.bfloat16),
             pltpu.SemaphoreType.DMA((depth,)),

time: 42.6 us -> 39.7 us (0.932)
  Pallas kernels: 41 us -> 38.1 us
    pallas_call x1, Pallas kernels: 41 us -> 38.1 us  [per_device(): pl.pallas_call(functools.partial(kernel, shards, cores, (kg, ng, kd, nd,...]
where the time goes in v3:
time: 39.7 us; the launch traced here: 39.5 us
  Pallas kernels  38.1 us (96%)
  local copies, waits for them, and re-layouts  1.36 us (3%)
    pallas_call x1, Pallas kernels, per_device(): pl.pallas_call(functools.partial(kernel, shards, cores, (kg, ng, kd, nd,...  38.1 us
    unnamed x1, local copies, waits for them, and re-layouts  1.36 us

profile of v3, /device:TPU:0, one launch (start us, length us, event | category | flops | bytes accessed | tf_op | source)
XLA Modules:
  0.0 39.5 jit_solution(7502162463850094790)
XLA Ops:
  0.0 38.1 %shard_map.64 = bf16[2,6144]{1,0:T(2,128)(2,1)} custom-call(s32[2,2]{1,0:T(2,128)} %ids_ref.1, f32[2,2]{1,0:T(2,128)} %mix_ref.1, bf16[2,6144]{1,0:T(2,128)(2,1)} %tok_ref.1, bf16[6144,2048]{1,0:T(8,128)(2,1)} %gate_ref.1, bf16[6144,2048]{1,0:T(8,128)(2,1)} %up_ref.1, bf16[2048,6144]{1,0:T(8,128)(2,1)} %down_ref.1), custom_call_target="tpu_custom_call" | custom-call | tf_op jit(solution)/shard_map/pallas_call | solution.py:285
  38.1 1.4 %copy.8 = bf16[2,6144]{1,0:T(2,128)(2,1)} copy(bf16[2,6144]{1,0:T(2,128)(2,1)} %shard_map.64) | data formatting | bytes 49152
